TPU v7x, 256 devices: a 8x8x2 block of a 8x8x16 slice. The times are simulated.
256 devices in a mesh: groups: 2 (over z), patch: 128 (over x, y, core).
Axes of the slice: x: 8, y: 8, z: 2, core: 2. Of those that a mesh axis runs over, the one named last changes fastest.
The devices are a block of a 8x8x16 slice.
Arguments:
- queries: bfloat16 [8192, 1536], P(('groups', 'patch')), parts along dimension 0, may hold values from -8 to 8
- fresh_keys: bfloat16 [8192, 1536], P(('groups', 'patch')), parts along dimension 0, may hold values from -8 to 8
- fresh_values: bfloat16 [8192, 1536], P(('groups', 'patch')), parts along dimension 0, may hold values from -128 to 128
- stale_keys: bfloat16 [8192, 1536], P(('groups', 'patch')), parts along dimension 0, may hold values from -8 to 8
- stale_values: bfloat16 [8192, 1536], P(('groups', 'patch')), parts along dimension 0, may hold values from -128 to 128
- text_keys: bfloat16 [452, 1536], P('groups'), parts along dimension 0, may hold values from -8 to 8
- text_values: bfloat16 [452, 1536], P('groups'), parts along dimension 0, may hold values from -128 to 128
- out_weight: bfloat16 [1536, 3072], P(None, 'patch'), may hold values from -0.15625 to 0.15625
- gate_table: float32 [50, 3072], replicated, may hold values from 0.1 to 1.9
- timestep: int32 [2], P('groups'), parts along dimension 0, may hold values from 0 to 49
Outputs:
- branch: bfloat16 [8192, 3072], P(('groups', 'patch')), parts along dimension 0
There are 2 independent parts, one for each index of `groups`. A program takes and returns all parts, laid end to end along the dimension named above; an argument that names none is the same for every part. Nothing has to cross between parts.
All inputs are finite; a program needn't handle non-finite values.
Results may differ from a plain program's by a relative error of at most 0.0095.
Values may be sent and summed in bfloat16 or wider, within the bound.
A program may use at most 128 MiB of HBM per device.

v0:
```python
import jax
import jax.numpy as jnp
from jax import lax
from jax.sharding import PartitionSpec as P

HEAD_DIM = 64
HEADS = 24


def sent_together(arrays, axis, dim, along):
    ends, at = ([], 0)
    for a in arrays[:-1]:
        at += a.shape[along]
        ends.append(at)
    both = jnp.concatenate(arrays, axis=along)
    return tuple(jnp.split(lax.all_gather(both, axis, axis=dim, tiled=True), ends, axis=along))


def body(
    queries,
    fresh_keys,
    fresh_values,
    stale_keys,
    stale_values,
    text_keys,
    text_values,
    out_weight,
    gate_table,
    timestep,
):
    row_count = queries.shape[0]
    head_count = HEADS
    head_width = HEAD_DIM
    scaling = head_width ** (-0.5)
    query = queries.reshape(row_count, head_count, head_width)

    def scores_for(key_block):
        shaped = key_block.reshape(key_block.shape[0], head_count, head_width)
        return (
            jnp.einsum("thd,shd->ths", query, shaped, preferred_element_type=jnp.float32) * scaling
        )

    def weigh(expo, value_block):
        shaped = value_block.reshape(value_block.shape[0], head_count, head_width)
        return jnp.einsum(
            "ths,shd->thd", expo.astype(jnp.bfloat16), shaped, preferred_element_type=jnp.float32
        )

    near_keys = jnp.concatenate([text_keys, fresh_keys], 0)
    near_values = jnp.concatenate([text_values, fresh_values], 0)
    near_scores = scores_for(near_keys)
    running_max = jnp.max(near_scores, -1)
    near_expo = jnp.exp(near_scores - running_max[..., None])
    running_sum = jnp.sum(near_expo, -1)
    weighted = weigh(near_expo, near_values)
    own_first = lax.axis_index("patch") * row_count
    key_part, value_part = sent_together((stale_keys, stale_values), "patch", 0, 1)
    positions = jnp.arange(key_part.shape[0], dtype=jnp.int32)
    remote_mask = (positions < own_first) | (positions >= own_first + row_count)
    scores = jnp.where(remote_mask[None, None, :], scores_for(key_part), -1e30)
    new_max = jnp.maximum(running_max, jnp.max(scores, -1))
    shrink = jnp.exp(running_max - new_max)
    expo = jnp.exp(scores - new_max[..., None])
    new_sum = running_sum * shrink + jnp.sum(expo, -1)
    new_weighted = weighted * shrink[..., None] + weigh(expo, value_part)
    attended = (
        (new_weighted / new_sum[..., None])
        .reshape(row_count, head_count * head_width)
        .astype(jnp.bfloat16)
    )
    projected = jnp.dot(
        attended,
        lax.all_gather(out_weight, "patch", axis=1, tiled=True),
        preferred_element_type=jnp.float32,
    )
    selector = (jnp.arange(gate_table.shape[0], dtype=jnp.int32) == timestep[0]).astype(jnp.float32)
    gating = jnp.dot(selector, gate_table, precision=lax.Precision.HIGHEST)
    return (projected * gating[None, :]).astype(jnp.bfloat16)


def solution(mesh):
    in_specs = (
        P(("groups", "patch"), None),
        P(("groups", "patch"), None),
        P(("groups", "patch"), None),
        P(("groups", "patch"), None),
        P(("groups", "patch"), None),
        P("groups", None),
        P("groups", None),
        P(None, "patch"),
        P(),
        P("groups"),
    )
    out_specs = P(("groups", "patch"), None)
    return jax.shard_map(body, mesh=mesh, in_specs=in_specs, out_specs=out_specs, check_vma=False)
```

profile of v0, /device:TPU:513, one launch (start us, length us, event | category | flops | bytes accessed | tf_op | source)
XLA Modules:
  0.0 246.7 jit_solution(3291035466819410238)
XLA Ops:
  6.5 0.0 copy-start
  6.6 0.0 all-gather.3.cloned.1.call-start
  6.6 1.7 pad_maximum_fusion.2
  8.3 0.1 all-gather.3.cloned.1.call-update
  8.3 0.1 all-gather.5.cloned.1.call-start
  8.4 0.7 all-gather.5.cloned.1.call-update
  9.1 1.1 reshape.49
  10.2 1.2 pad_maximum_fusion.1
  11.4 0.7 copy.18
  12.2 1.2 pad_maximum_fusion
  13.4 1.4 copy.17
  15.5 0.4 fusion.34
  15.9 0.4 fusion.18
  16.3 0.0 copy-done
  16.3 0.3 fusion.26
  16.6 129.8 %all-gather.3.cloned.1.call-done = bf16[4096,3072]{1,0:T(8,128)(2,1)} async-done(((bf16[32,3072]{1,0:T(8,128)(2,1)}), bf16[4096,3072]{1,0:T(8,128)(2,1)}) %all-gather.3.cloned.1.call-update) | async-done | bytes 25165840 | tf_op jit(solution)/shard_map/all_gather | solution.py:16
  146.4 17.1 %fusion.33 = (bf16[4096,1536]{1,0:T(8,128)(2,1)}, bf16[4096,1536]{1,0:T(8,128)(2,1)}) fusion(bf16[4096,3072]{1,0:T(8,128)(2,1)} %all-gather.3.cloned.1.call-done), kind=kLoop, calls=%fused_computation.43 | loop fusion | bytes 50331648 | tf_op jit(solution)/shard_map/split | solution.py:16
  163.5 16.4 %copy.22 = bf16[4096,1536]{0,1:T(8,128)(2,1)} copy(bf16[4096,1536]{1,0:T(8,128)(2,1)} %get-tuple-element.8) | data formatting | bytes 25165824 | tf_op jit(solution)/shard_map/split | solution.py:16
  179.9 16.8 %copy.20 = bf16[4096,1536]{0,1:T(8,128)(2,1)} copy(bf16[4096,1536]{1,0:T(8,128)(2,1)} %get-tuple-element.7) | data formatting | bytes 25165824 | tf_op jit(solution)/shard_map/split | solution.py:16
  196.7 6.4 %bitcast_reduce_fusion = (f32[32,24]{0,1:T(8,128)S(1)}, f32[24,4096,32]{1,2,0:T(8,128)S(1)}) fusion(pred[4096]{0:T(1024)(128)(4,1)S(1)} %fusion.25, bf16[4096,24,64]{0,2,1:T(8,128)(2,1)} %bitcast.43, bf16[32,24,64]{2,1,0:T(8,128)(2,1)S(1)} %reshape.49), kind=kOutput, calls=%fused_computation.1 | convolution fusion | flops 412089600 | bytes 25271296 | tf_op jit(solution)/shard_map/thd,shd->ths/dot_general | solution.py:40
  203.1 0.0 copy-start.2
  203.1 4.6 %copy-done.2 = f32[24,4096,32]{1,2,0:T(8,128)} copy-done((f32[24,4096,32]{1,2,0:T(8,128)}, f32[24,4096,32]{1,2,0:T(8,128)S(1)}, u32[]{:S(2)}) %copy-start.2) | copy-done | bytes 12582936
  207.7 3.0 %fusion.1 = f32[32,24]{0,1:T(8,128)S(1)} fusion(f32[24,4096,32]{1,2,0:T(8,128)S(1)} %get-tuple-element.12, f32[32,24]{0,1:T(8,128)S(1)} %max.13, pred[4096]{0:T(1024)(128)(4,1)S(1)} %fusion.25), kind=kLoop, calls=%fused_computation.4 | loop fusion | flops 12582144 | bytes 12593152 | tf_op jit(solution)/shard_map/reduce_sum | solution.py:64
  210.8 0.0 copy-start.3
  210.8 0.0 copy-start.1
  210.8 11.1 %fusion.14 = f32[32,24,64]{2,0,1:T(8,128)S(1)} fusion(bf16[4096,24,64]{0,2,1:T(8,128)(2,1)} %bitcast.44, f32[24,4096,32]{1,2,0:T(8,128)} %copy-done.2, f32[32,24]{0,1:T(8,128)S(1)} %max.13, pred[4096]{0:T(1024)(128)(4,1)S(1)} %fusion.25), kind=kOutput, calls=%fused_computation.19 | convolution fusion | flops 415236096 | bytes 25369600 | tf_op jit(solution)/shard_map/ths,shd->thd/dot_general | solution.py:45
  221.9 0.0 copy-done.3
  221.9 0.6 fusion.17
  222.5 0.1 copy.23
  222.6 0.2 convert_element_type.19
  222.8 9.8 %all-gather.5.cloned.1.call-done = bf16[1536,3072]{0,1:T(8,128)(2,1)} async-done(((bf16[1536,24]{0,1:T(8,128)(2,1)}), bf16[1536,3072]{0,1:T(8,128)(2,1)}) %all-gather.5.cloned.1.call-update) | async-done | bytes 9437200 | tf_op jit(solution)/shard_map/all_gather | solution.py:73
  232.6 7.2 %fusion.9 = bf16[32,3072]{1,0:T(8,128)(2,1)} fusion(bf16[32,1536]{1,0:T(8,128)(2,1)S(1)} %convert_element_type.19, bf16[1536,3072]{0,1:T(8,128)(2,1)} %all-gather.5.cloned.1.call-done, f32[3072]{0:T(1024)S(1)} %bitcast.47), kind=kOutput, calls=%fused_computation.12 | convolution fusion | flops 302186496 | bytes 9744384 | tf_op jit(solution)/shard_map/dot_general | solution.py:71
  239.8 0.0 copy-done.1
  (3 shorter events, 0.0 us)
Async XLA Ops:
  6.5 9.7 %copy-start = (f32[50,3072]{1,0:T(8,128)S(1)}, f32[50,3072]{1,0:T(8,128)}, u32[]{:S(2)}) copy-start(f32[50,3072]{1,0:T(8,128)} %param.18) | copy-start | bytes 1843204
  6.6 139.9 %all-gather.3.cloned.1.call-start = ((), (), s32[]{:S(2)}) async-start(), calls=%async_computation | async-start | bytes 25362432 | tf_op jit(solution)/shard_map/all_gather | solution.py:16
  8.3 224.3 %all-gather.5.cloned.1.call-start = ((), (), s32[]{:S(2)}) async-start(), calls=%async_computation.1 | async-start | bytes 9510912 | tf_op jit(solution)/shard_map/all_gather | solution.py:73
  203.1 4.6 %copy-start.2 = (f32[24,4096,32]{1,2,0:T(8,128)}, f32[24,4096,32]{1,2,0:T(8,128)S(1)}, u32[]{:S(2)}) copy-start(f32[24,4096,32]{1,2,0:T(8,128)S(1)} %get-tuple-element.12) | copy-start | bytes 37748740
  210.8 11.2 %copy-start.3 = (bf16[258,1536]{0,1:T(8,128)(2,1)S(1)}, bf16[258,1536]{0,1:T(8,128)(2,1)}, u32[]{:S(2)}) copy-start(bf16[258,1536]{0,1:T(8,128)(2,1)} %copy.17) | copy-start | bytes 2377732
  210.8 29.1 %copy-start.1 = (f32[50,3072]{1,0:T(8,128)S(1)}, f32[50,3072]{1,0:T(8,128)}, u32[]{:S(2)}) copy-start(f32[50,3072]{1,0:T(8,128)} %param.18) | copy-start | bytes 1843204
Sparse Core Ops, SparseCore 0:
  9.9 136.4 all-gather.2
  149.0 83.5 all-gather.4
where the time goes:
time: 248 us; the launch traced here: 247 us
  waiting for transfers between devices  140 us (56%)
  local copies, waits for them, and re-layouts  58.3 us (24%)
  matrix products  26.1 us (11%)
  between operations  14.2 us (6%)
  other arithmetic  7.58 us (3%)
    all_gather x1, waiting for transfers between devices, sent_together(): lax.all_gather(both, axis, axis=dim, tiled=True)  130 us
    split x3, local copies, waits for them, and re-layouts, sent_together(): jnp.split(lax.all_gather(both, axis, axis=dim, tiled=True), ends, axis=al...  50.3 us
    dot_general x2, matrix products, weigh(): jnp.einsum('ths,shd->thd', expo.astype(jnp.bfloat16), shaped, preferred_e...  11.7 us
    all_gather x1, waiting for transfers between devices, body(): lax.all_gather(out_weight, 'patch', axis=1, tiled=True)  9.83 us
    dot_general x1, matrix products, body(): jnp.dot(attended, lax.all_gather(out_weight, 'patch', axis=1, tiled=True)...  7.19 us
    dot_general x2, matrix products, scores_for(): jnp.einsum('thd,shd->ths', query, shaped, preferred_element_type=jnp.floa...  6.84 us
  transfers between devices with their start and end apart: 2, of which 2 were waited for; matrix products, arithmetic and copies ran while one was open for 32% of the time, Pallas kernels for 0%

commit v1 on v0

--- a/solution.py
+++ b/solution.py
@@ -70,7 +70,9 @@
     )
     projected = jnp.dot(
         attended,
-        lax.all_gather(out_weight, "patch", axis=1, tiled=True),
+        jnp.concatenate(
+            lax.all_to_all(jnp.stack([out_weight] * lax.axis_size("patch")), "patch", 0, 0), axis=1
+        ),
         preferred_element_type=jnp.float32,
     )
     selector = (jnp.arange(gate_table.shape[0], dtype=jnp.int32) == timestep[0]).astype(jnp.float32)

time: 248 us -> 475 us (1.92)
  waiting for transfers between devices: 140 us -> 338 us
  starting transfers between devices: 0.07 us -> 28.5 us
    all_gather x1, waiting for transfers between devices: 130 us -> 338 us  [sent_together(): lax.all_gather(both, axis, axis=dim, tiled=True)]
    all_to_all x0 -> x1, starting transfers between devices: none -> 28.5 us  [body(): lax.all_to_all(jnp.stack([out_weight] * lax.axis_size('patch')), 'patch',...]
    all_gather x1 -> x0, waiting for transfers between devices: 9.83 us -> none  [body(): lax.all_gather(out_weight, 'patch', axis=1, tiled=True)]
    another operation x0 -> x1, local copies, waits for them, and re-layouts: none -> 5.11 us  [body(): jnp.stack([out_weight] * lax.axis_size('patch'))]
  transfers between devices with their start and end apart: 2 -> 2, of which waited for: 2 -> 1; matrix products, arithmetic and copies ran while one was open for 32% -> 17% of each run, Pallas kernels for 0% -> 0%
where the time goes in v1:
time: 475 us; the launch traced here: 474 us
  waiting for transfers between devices  338 us (71%)
  local copies, waits for them, and re-layouts  62.7 us (13%)
  starting transfers between devices  28.5 us (6%)
  matrix products  24.8 us (5%)
  between operations  14.3 us (3%)
  other arithmetic  6.38 us (1%)
    all_gather x1, waiting for transfers between devices, sent_together(): lax.all_gather(both, axis, axis=dim, tiled=True)  338 us
    split x3, local copies, waits for them, and re-layouts, sent_together(): jnp.split(lax.all_gather(both, axis, axis=dim, tiled=True), ends, axis=al...  50.5 us
    all_to_all x1, starting transfers between devices, body(): lax.all_to_all(jnp.stack([out_weight] * lax.axis_size('patch')), 'patch',...  28.5 us
    dot_general x2, matrix products, weigh(): jnp.einsum('ths,shd->thd', expo.astype(jnp.bfloat16), shaped, preferred_e...  10.8 us
  transfers between devices with their start and end apart: 2, of which 1 were waited for; matrix products, arithmetic and copies ran while one was open for 17% of the time, Pallas kernels for 0%

profile of v1, /device:TPU:513, one launch (start us, length us, event | category | flops | bytes accessed | tf_op | source)
XLA Modules:
  0.0 474.3 jit_solution(1568323492249783316)
XLA Ops:
  6.5 0.0 copy-start
  6.6 0.0 all-gather.2.cloned.1.call-start
  6.6 1.7 pad_maximum_fusion.2
  8.3 0.1 all-gather.2.cloned.1.call-update
  8.3 0.0 copy-start.7
  8.3 0.0 copy-start.4
  8.3 0.0 copy-start.5
  8.3 5.1 %stack.2 = bf16[128,1536,24]{1,2,0:T(8,128)(2,1)} broadcast(bf16[1536,24]{0,1:T(8,128)(2,1)} %param.17), dimensions={1,2} | broadcast | bytes 9510912 | tf_op jit(solution)/shard_map/stack | solution.py:74
  13.5 0.0 copy-start.6
  13.5 28.5 %all-to-all-start = ((bf16[128,1536,24]{1,2,0:T(8,128)(2,1)}), bf16[128,1536,24]{1,2,0:T(8,128)(2,1)}, u32[]{:S(2)}, u32[]{:S(2)}) async-start(bf16[128,1536,24]{1,2,0:T(8,128)(2,1)} %stack.2), calls=%async_computation | async-start | bytes 18874368 | tf_op jit(solution)/shard_map/all_to_all | solution.py:74
  42.0 0.0 copy-done.7
  42.0 0.2 reshape.57
  42.1 0.0 copy-done.4
  42.2 0.0 copy-done.5
  42.2 0.1 pad_maximum_fusion.1
  42.2 0.7 copy.19
  43.0 0.0 copy-done.6
  43.0 1.2 pad_maximum_fusion
  44.2 1.4 copy.18
  46.2 0.4 fusion.34
  46.6 0.4 fusion.18
  47.0 0.0 copy-done
  47.0 0.3 fusion.26
  47.4 337.7 %all-gather.2.cloned.1.call-done = bf16[4096,3072]{1,0:T(8,128)(2,1)} async-done(((bf16[32,3072]{1,0:T(8,128)(2,1)}), bf16[4096,3072]{1,0:T(8,128)(2,1)}) %all-gather.2.cloned.1.call-update) | async-done | bytes 25165840 | tf_op jit(solution)/shard_map/all_gather | solution.py:16
  385.1 17.1 %fusion.33 = (bf16[4096,1536]{1,0:T(8,128)(2,1)}, bf16[4096,1536]{1,0:T(8,128)(2,1)}) fusion(bf16[4096,3072]{1,0:T(8,128)(2,1)} %all-gather.2.cloned.1.call-done), kind=kLoop, calls=%fused_computation.43 | loop fusion | bytes 50331648 | tf_op jit(solution)/shard_map/split | solution.py:16
  402.2 16.6 %copy.23 = bf16[4096,1536]{0,1:T(8,128)(2,1)} copy(bf16[4096,1536]{1,0:T(8,128)(2,1)} %get-tuple-element.8) | data formatting | bytes 25165824 | tf_op jit(solution)/shard_map/split | solution.py:16
  418.8 16.8 %copy.21 = bf16[4096,1536]{0,1:T(8,128)(2,1)} copy(bf16[4096,1536]{1,0:T(8,128)(2,1)} %get-tuple-element.7) | data formatting | bytes 25165824 | tf_op jit(solution)/shard_map/split | solution.py:16
  435.6 6.0 %bitcast_reduce_fusion = (f32[32,24]{0,1:T(8,128)S(1)}, f32[24,4096,32]{1,2,0:T(8,128)S(1)}) fusion(pred[4096]{0:T(1024)(128)(4,1)S(1)} %fusion.25, bf16[4096,24,64]{0,2,1:T(8,128)(2,1)} %bitcast.46, bf16[32,24,64]{2,1,0:T(8,128)(2,1)S(1)} %reshape.57), kind=kOutput, calls=%fused_computation.1 | convolution fusion | flops 412089600 | bytes 25271296 | tf_op jit(solution)/shard_map/thd,shd->ths/dot_general | solution.py:40
  441.6 0.0 copy-start.2
  441.6 4.5 copy-done.2
  446.1 3.0 fusion.1
  449.1 0.0 copy-start.3
  449.1 0.0 copy-start.1
  449.1 10.1 %fusion.14 = f32[32,24,64]{2,0,1:T(8,128)S(1)} fusion(bf16[4096,24,64]{0,2,1:T(8,128)(2,1)} %bitcast.47, f32[24,4096,32]{1,2,0:T(8,128)} %copy-done.2, f32[32,24]{0,1:T(8,128)S(1)} %max.13, pred[4096]{0:T(1024)(128)(4,1)S(1)} %fusion.25), kind=kOutput, calls=%fused_computation.19 | convolution fusion | flops 415236096 | bytes 25369600 | tf_op jit(solution)/shard_map/ths,shd->thd/dot_general | solution.py:45
  459.3 0.0 copy-done.3
  459.3 0.6 fusion.17
  459.9 0.1 copy.24
  460.0 0.2 convert_element_type.19
  460.2 0.0 all-to-all-done
  460.2 7.2 %fusion.9 = bf16[32,3072]{1,0:T(8,128)(2,1)} fusion(bf16[32,1536]{1,0:T(8,128)(2,1)S(1)} %convert_element_type.19, bf16[1536,3072]{0,1:T(8,128)(2,1)} %bitcast.9, f32[3072]{0:T(1024)S(1)} %bitcast.50), kind=kOutput, calls=%fused_computation.12 | convolution fusion | flops 302186496 | bytes 9744384 | tf_op jit(solution)/shard_map/dot_general | solution.py:71
  467.4 0.0 copy-done.1
  (3 shorter events, 0.0 us)
Async XLA Ops:
  6.5 40.5 %copy-start = (f32[50,3072]{1,0:T(8,128)S(1)}, f32[50,3072]{1,0:T(8,128)}, u32[]{:S(2)}) copy-start(f32[50,3072]{1,0:T(8,128)} %param.18) | copy-start | bytes 1843204
  6.6 378.5 %all-gather.2.cloned.1.call-start = ((), (), s32[]{:S(2)}) async-start(), calls=%async_computation.1 | async-start | bytes 25362432 | tf_op jit(solution)/shard_map/all_gather | solution.py:16
  8.3 33.7 %copy-start.7 = (bf16[32,1536]{1,0:T(8,128)(2,1)S(1)}, bf16[32,1536]{1,0:T(8,128)(2,1)}, u32[]{:S(2)}) copy-start(bf16[32,1536]{1,0:T(8,128)(2,1)} %param.10) | copy-start | bytes 294916
  8.3 33.8 %copy-start.4 = (bf16[226,1536]{1,0:T(8,128)(2,1)S(1)}, bf16[226,1536]{1,0:T(8,128)(2,1)}, u32[]{:S(2)}) copy-start(bf16[226,1536]{1,0:T(8,128)(2,1)} %param.15) | copy-start | bytes 2082820
  8.3 33.8 %copy-start.5 = (bf16[32,1536]{1,0:T(8,128)(2,1)S(1)}, bf16[32,1536]{1,0:T(8,128)(2,1)}, u32[]{:S(2)}) copy-start(bf16[32,1536]{1,0:T(8,128)(2,1)} %param.11) | copy-start | bytes 294916
  13.5 29.5 %copy-start.6 = (bf16[32,1536]{1,0:T(8,128)(2,1)S(1)}, bf16[32,1536]{1,0:T(8,128)(2,1)}, u32[]{:S(2)}) copy-start(bf16[32,1536]{1,0:T(8,128)(2,1)} %param.12) | copy-start | bytes 294916
  13.5 446.7 %all-to-all-start = ((bf16[128,1536,24]{1,2,0:T(8,128)(2,1)}), bf16[128,1536,24]{1,2,0:T(8,128)(2,1)}, u32[]{:S(2)}, u32[]{:S(2)}) async-start(bf16[128,1536,24]{1,2,0:T(8,128)(2,1)} %stack.2), calls=%async_computation | async-start | bytes 18874368 | tf_op jit(solution)/shard_map/all_to_all | solution.py:74
  441.6 4.5 copy-start.2
  449.1 10.2 %copy-start.3 = (bf16[258,1536]{0,1:T(8,128)(2,1)S(1)}, bf16[258,1536]{0,1:T(8,128)(2,1)}, u32[]{:S(2)}) copy-start(bf16[258,1536]{0,1:T(8,128)(2,1)} %copy.18) | copy-start | bytes 2377732
  449.1 18.3 %copy-start.1 = (f32[50,3072]{1,0:T(8,128)S(1)}, f32[50,3072]{1,0:T(8,128)}, u32[]{:S(2)}) copy-start(f32[50,3072]{1,0:T(8,128)} %param.18) | copy-start | bytes 1843204
Sparse Core Ops, SparseCore 0:
  9.9 375.0 all-gather.1
